TPU v7x, 32 devices: a whole 2x2x4 slice. The times are simulated.
32 devices in a mesh: gx: 8 (over z, y), gy: 4 (over x, core).
Axes of the slice: x: 2, y: 2, z: 4, core: 2. Of those that a mesh axis runs over, the one named last changes fastest.
Arguments:
- three_index: bfloat16 [8, 4608, 4608], P('gx', 'gy'), as said below
- old_density: bfloat16 [4608, 4608], P('gy'), as said below
- core: float32 [4608, 4608], P('gy', 'gx'), as said below
Outputs:
- purified: bfloat16 [4608, 4608], P('gy', 'gx')
- idempotency: float32 [2], replicated
Inputs may be any that keep to these rules, and one draw needn't show every extreme that they name: Each slab three_index[P] is symmetric in its two basis indices. `old_density`: symmetric. `core`: symmetric.
All inputs are finite; a program needn't handle non-finite values.
Results may differ from a plain program's by a relative error of at most 0.015.
Values may be sent and summed in bfloat16 or wider, within the bound.
A program may use at most 128 MiB of HBM per device.

v0:
```python
import jax
import jax.numpy as jnp
from jax import lax
from jax.sharding import PartitionSpec as P

ITERS = 2


def per_device(three_index, old_density, core):
    aux_dev, rows, width = three_index.shape
    cols = core.shape[1]
    flat = three_index.reshape(aux_dev, rows * width)
    partial_value = jnp.dot(
        flat, old_density.reshape(rows * width), preferred_element_type=jnp.float32
    )
    fitted = lax.psum(partial_value, "gy")
    fitted16 = fitted.astype(jnp.bfloat16)
    coulomb = lax.psum_scatter(
        jnp.einsum("p,prc->cr", fitted16, three_index, preferred_element_type=jnp.float32).astype(
            jnp.bfloat16
        ),
        "gx",
        scatter_dimension=0,
        tiled=True,
    ).astype(jnp.float32)
    fock = core + coulomb.T
    row_start = lax.axis_index("gy") * rows
    col_start = lax.axis_index("gx") * cols
    row_ids = row_start + lax.broadcasted_iota(jnp.int32, (rows, cols), 0)
    col_ids = col_start + lax.broadcasted_iota(jnp.int32, (rows, cols), 1)
    diag_mask = (row_ids == col_ids).astype(jnp.float32)
    local_trace = jnp.sum(fock * diag_mask)
    shift = lax.psum(local_trace, ("gx", "gy")) / width
    shifted = fock - shift * diag_mask
    spread = lax.psum(jnp.sum(shifted * shifted), ("gx", "gy")) / (width * width)
    current = ((shift * diag_mask - fock) / (4.0 * jnp.sqrt(spread + 1e-06))).astype(jnp.bfloat16)
    scale = 1.0 / jnp.sqrt(jnp.float32(width))
    traces = []
    for step in range(ITERS):
        right = lax.all_gather(current, "gy", axis=0, tiled=True)
        row_panel = lax.all_gather(current, "gx", axis=1, tiled=True)
        square_full = jnp.dot(row_panel, right, preferred_element_type=jnp.float32) * scale
        square = square_full.astype(jnp.bfloat16)
        square_block = lax.all_gather(square, "gy", axis=0, tiled=True)
        cube = jnp.dot(row_panel, square_block, preferred_element_type=jnp.float32) * scale
        traces.append(jnp.sum(square_full * diag_mask))
        current = (1.5 * current.astype(jnp.float32) - 2.0 * cube).astype(jnp.bfloat16)
    totals = lax.psum(jnp.stack(traces), ("gx", "gy"))
    idempotency = 16.0 * (0.25 - totals / (width * jnp.sqrt(jnp.float32(width))))
    return (current, idempotency)


def solution(mesh):
    placed = (P("gx", "gy", None), P("gy", None), P("gy", "gx"))
    return jax.shard_map(
        per_device, mesh=mesh, in_specs=placed, out_specs=(P("gy", "gx"), P()), check_vma=False
    )
```

profile of v0, /device:TPU:0, one launch (start us, length us, event | category | flops | bytes accessed | tf_op | source)
XLA Modules:
  0.0 895.6 jit_solution(16187595499375123604)
XLA Ops:
  7.2 0.0 reduce-scatter.2.cloned.1.call-start
  7.2 19.8 %reshape.23 = bf16[5308416]{0:T(1024)(128)(2,1)} reshape(bf16[1,1152,4608]{2,1,0:T(8,128)(2,1)} %param.3) | data formatting | bytes 21233664 | tf_op jit(solution)/shard_map/reshape
  27.0 15.3 %copy.5 = bf16[1,1152,4608]{1,2,0:T(8,128)(2,1)} copy(bf16[1,1152,4608]{2,1,0:T(8,128)(2,1)} %param.3) | data formatting | bytes 21233664 | tf_op args[0]
  42.3 19.8 %reshape.24 = bf16[5308416]{0:T(1024)(128)(2,1)} reshape(bf16[1152,4608]{1,0:T(8,128)(2,1)} %param.4) | data formatting | bytes 21233664 | tf_op jit(solution)/shard_map/reshape | solution.py:14
  62.1 10.9 %fusion = f32[]{:T(128)} fusion(bf16[5308416]{0:T(1024)(128)(2,1)} %reshape.23, bf16[5308416]{0:T(1024)(128)(2,1)} %reshape.24), kind=kLoop, calls=%fused_computation.1 | loop fusion | flops 21233664 | bytes 21233668 | tf_op jit(solution)/shard_map/dot_general | solution.py:13
  72.9 9.0 %psum.28 = bf16[1]{0:T(256)(128)(2,1)} all-reduce(f32[1]{0:T(128)} %bitcast), channel_id=1, replica_groups=mesh['gx'=8,'gy'=4] {'gy'}, use_global_device_ids=true, to_apply=%region_0.0 | all-reduce | flops 1 | bytes 6 | tf_op jit(solution)/shard_map/psum | solution.py:16
  82.6 10.5 %fusion.1 = bf16[4608,1152]{1,0:T(8,128)(2,1)} fusion(bf16[1,1152,4608]{1,2,0:T(8,128)(2,1)} %copy.5, f32[]{:T(128)S(6)} %convert.13), kind=kLoop, calls=%fused_computation.3 | loop fusion | flops 15925248 | bytes 21233668 | tf_op jit(solution)/shard_map/convert_element_type | solution.py:19
  93.1 0.0 copy-start
  93.1 0.0 reduce-scatter.2.cloned.1.call-update
  93.1 0.0 all-gather.9.cloned.1.call-start
  93.2 180.8 %reduce-scatter.2.cloned.1.call-done = bf16[576,1152]{1,0:T(8,128)(2,1)} async-done(((bf16[4608,1152]{1,0:T(8,128)(2,1)}), bf16[576,1152]{1,0:T(8,128)(2,1)}) %reduce-scatter.2.cloned.1.call-update) | async-done | bytes 1327120 | tf_op jit(solution)/shard_map/reduce_scatter | solution.py:18
  274.1 0.0 copy-done
  274.1 2.8 fusion.11
  276.9 39.5 %psum.29 = f32[]{:T(128)} all-reduce(f32[]{:T(128)} %fusion.11), channel_id=1, replica_groups=mesh['gx'=8,'gy'=4] {'gx','gy'}, use_global_device_ids=true, to_apply=%region_3.0 | all-reduce | flops 1 | bytes 8 | tf_op jit(solution)/shard_map/psum | solution.py:33
  317.0 2.9 fusion.10
  319.9 40.2 %psum.30 = f32[]{:T(128)} all-reduce(f32[]{:T(128)} %fusion.10), channel_id=1, replica_groups=mesh['gx'=8,'gy'=4] {'gx','gy'}, use_global_device_ids=true, to_apply=%region_5.0 | all-reduce | flops 1 | bytes 8 | tf_op jit(solution)/shard_map/psum | solution.py:35
  360.8 3.0 fusion.14
  363.8 0.0 all-gather.9.cloned.1.call-update
  363.8 0.0 all-gather.7.cloned.1.call-start
  363.9 0.7 all-gather.7.cloned.1.call-update
  364.6 0.0 copy-start.1
  364.6 0.0 all-gather.11.cloned.1.call-start
  364.6 40.2 %all-gather.9.cloned.1.call-done = bf16[4608,576]{0,1:T(8,128)(2,1)} async-done(((bf16[1152,576]{0,1:T(8,128)(2,1)}), bf16[4608,576]{0,1:T(8,128)(2,1)}) %all-gather.9.cloned.1.call-update) | async-done | bytes 5308432 | tf_op jit(solution)/shard_map/all_gather | solution.py:40
  404.9 154.9 %all-gather.7.cloned.1.call-done = bf16[1152,4608]{0,1:T(8,128)(2,1)} async-done(((bf16[1152,576]{0,1:T(8,128)(2,1)}), bf16[1152,4608]{0,1:T(8,128)(2,1)}) %all-gather.7.cloned.1.call-update) | async-done | bytes 10616848 | tf_op jit(solution)/shard_map/all_gather | solution.py:41
  559.8 13.3 %fusion.15 = (bf16[1152,576]{0,1:T(8,128)(2,1)}, f32[1152,576]{0,1:T(8,128)}) fusion(bf16[4608,576]{0,1:T(8,128)(2,1)} %all-gather.9.cloned.1.call-done, bf16[1152,4608]{0,1:T(8,128)(2,1)} %all-gather.7.cloned.1.call-done), kind=kOutput, calls=%fused_computation.30 | convolution fusion | flops 6116622336 | bytes 19906560 | tf_op jit(solution)/shard_map/dot_general | solution.py:42
  573.1 0.0 all-gather.11.cloned.1.call-update
  573.1 0.2 all-gather.15.cloned.1.call-start
  573.4 38.9 %all-gather.11.cloned.1.call-done = bf16[4608,576]{0,1:T(8,128)(2,1)} async-done(((bf16[1152,576]{0,1:T(8,128)(2,1)}), bf16[4608,576]{0,1:T(8,128)(2,1)}) %all-gather.11.cloned.1.call-update) | async-done | bytes 5308432 | tf_op jit(solution)/shard_map/all_gather | solution.py:44
  612.2 0.0 copy-done.1
  612.2 12.9 %fusion.7 = bf16[1152,576]{0,1:T(8,128)(2,1)} fusion(bf16[4608,576]{0,1:T(8,128)(2,1)} %all-gather.11.cloned.1.call-done, bf16[1152,4608]{0,1:T(8,128)(2,1)} %all-gather.7.cloned.1.call-done, bf16[1152,576]{0,1:T(8,128)(2,1)S(1)} %copy-done.1), kind=kOutput, calls=%fused_computation.17 | convolution fusion | flops 6118612992 | bytes 18579456 | tf_op jit(solution)/shard_map/dot_general | solution.py:45
  625.1 0.0 all-gather.15.cloned.1.call-update
  625.1 0.0 all-gather.13.cloned.1.call-start
  625.2 0.5 all-gather.13.cloned.1.call-update
  625.7 0.0 all-gather.17.cloned.1.call-start
  625.7 40.3 %all-gather.15.cloned.1.call-done = bf16[4608,576]{0,1:T(8,128)(2,1)} async-done(((bf16[1152,576]{0,1:T(8,128)(2,1)}), bf16[4608,576]{0,1:T(8,128)(2,1)}) %all-gather.15.cloned.1.call-update) | async-done | bytes 5308432 | tf_op jit(solution)/shard_map/all_gather | solution.py:40
  666.0 154.8 %all-gather.13.cloned.1.call-done = bf16[1152,4608]{0,1:T(8,128)(2,1)} async-done(((bf16[1152,576]{0,1:T(8,128)(2,1)}), bf16[1152,4608]{0,1:T(8,128)(2,1)}) %all-gather.13.cloned.1.call-update) | async-done | bytes 10616848 | tf_op jit(solution)/shard_map/all_gather | solution.py:41
  820.8 0.0 copy-start.2
  820.8 14.1 %fusion.12 = (f32[]{:T(128)}, f32[]{:T(128)}, bf16[1152,576]{0,1:T(8,128)(2,1)}) fusion(f32[1152,576]{0,1:T(8,128)} %get-tuple-element.6, s32[1152]{0:T(1024)S(1)} %iota_add_fusion, s32[576]{0:T(1024)S(1)} %iota_add_fusion.1, bf16[4608,576]{0,1:T(8,128)(2,1)} %all-gather.15.cloned.1.call-done, bf16[1152,4608]{0,1:T(8,128)(2,1)} %all-gather.13.cloned.1.call-done), kind=kOutput, calls=%fused_computation.22 | convolution fusion | flops 6119940096 | bytes 19913480 | tf_op jit(solution)/shard_map/dot_general | solution.py:42
  834.9 0.0 all-gather.17.cloned.1.call-update
  834.9 1.4 pad_maximum_fusion
  836.3 39.1 %psum.31 = f32[2]{0:T(128)S(1)} all-reduce(f32[2]{0:T(128)S(1)} %pad_maximum_fusion), channel_id=1, replica_groups=mesh['gx'=8,'gy'=4] {'gx','gy'}, use_global_device_ids=true, to_apply=%region_8.0 | all-reduce | flops 2 | bytes 16 | tf_op jit(solution)/shard_map/psum | solution.py:48
  875.4 0.5 subtract_multiply_fusion
  875.9 0.0 all-gather.17.cloned.1.call-done
  875.9 0.0 copy-done.2
  875.9 12.9 %fusion.6 = bf16[1152,576]{0,1:T(8,128)(2,1)} fusion(bf16[4608,576]{0,1:T(8,128)(2,1)} %all-gather.17.cloned.1.call-done, bf16[1152,4608]{0,1:T(8,128)(2,1)} %all-gather.13.cloned.1.call-done, bf16[1152,576]{0,1:T(8,128)(2,1)S(1)} %copy-done.2), kind=kOutput, calls=%fused_computation.16 | convolution fusion | flops 6118612992 | bytes 18579456 | tf_op jit(solution)/shard_map/dot_general | solution.py:45
  (2 shorter events, 0.0 us)
Async XLA Ops:
  7.2 266.9 %reduce-scatter.2.cloned.1.call-start = ((), (), s32[]{:S(2)}) async-start(), calls=%async_computation.1 | async-start | bytes 11943936 | tf_op jit(solution)/shard_map/reduce_scatter | solution.py:18
  93.1 181.0 %copy-start = (f32[1152,576]{0,1:T(8,128)S(1)}, f32[1152,576]{0,1:T(8,128)}, u32[]{:S(2)}) copy-start(f32[1152,576]{0,1:T(8,128)} %param.5) | copy-start | bytes 7962628
  93.1 311.7 %all-gather.9.cloned.1.call-start = ((), (), s32[]{:S(2)}) async-start(), calls=%async_computation.3 | async-start | bytes 6635520 | tf_op jit(solution)/shard_map/all_gather | solution.py:40
  363.8 196.0 %all-gather.7.cloned.1.call-start = ((), (), s32[]{:S(2)}) async-start(), calls=%async_computation.2 | async-start | bytes 11943936 | tf_op jit(solution)/shard_map/all_gather | solution.py:41
  364.6 247.7 %copy-start.1 = (bf16[1152,576]{0,1:T(8,128)(2,1)S(1)}, bf16[1152,576]{0,1:T(8,128)(2,1)}, u32[]{:S(2)}) copy-start(bf16[1152,576]{0,1:T(8,128)(2,1)} %fusion.14) | copy-start | bytes 3981316
  364.6 247.6 %all-gather.11.cloned.1.call-start = ((), (), s32[]{:S(2)}) async-start(), calls=%async_computation.4 | async-start | bytes 6635520 | tf_op jit(solution)/shard_map/all_gather | solution.py:44
  573.1 92.9 %all-gather.15.cloned.1.call-start = ((), (), s32[]{:S(2)}) async-start(), calls=%async_computation.6 | async-start | bytes 6635520 | tf_op jit(solution)/shard_map/all_gather | solution.py:40
  625.1 195.7 %all-gather.13.cloned.1.call-start = ((), (), s32[]{:S(2)}) async-start(), calls=%async_computation.5 | async-start | bytes 11943936 | tf_op jit(solution)/shard_map/all_gather | solution.py:41
  625.7 250.2 %all-gather.17.cloned.1.call-start = ((), (), s32[]{:S(2)}) async-start(), calls=%async_computation.7 | async-start | bytes 6635520 | tf_op jit(solution)/shard_map/all_gather | solution.py:44
  820.8 55.1 %copy-start.2 = (bf16[1152,576]{0,1:T(8,128)(2,1)S(1)}, bf16[1152,576]{0,1:T(8,128)(2,1)}, u32[]{:S(2)}) copy-start(bf16[1152,576]{0,1:T(8,128)(2,1)} %fusion.7) | copy-start | bytes 3981316
Sparse Core Ops, SparseCore 0:
  93.3 180.7 reduce-scatter.1
  363.9 40.8 all-gather.8
  407.6 152.1 all-gather.6
  573.3 38.9 all-gather.10
  625.2 40.7 all-gather.14
  668.6 152.1 all-gather.12
  835.0 39.4 all-gather.16
where the time goes:
time: 897 us; the launch traced here: 896 us
  waiting for transfers between devices  611 us (68%)
  blocking collectives  128 us (14%)
  local copies, waits for them, and re-layouts  54.9 us (6%)
  matrix products  53.1 us (6%)
  other arithmetic  32 us (4%)
  between operations  16.2 us (2%)
    all_gather x2, waiting for transfers between devices, per_device(): row_panel = lax.all_gather(current, 'gx', axis=1, tiled=True)  310 us
    reduce_scatter x1, waiting for transfers between devices, per_device(): lax.psum_scatter(jnp.einsum('p,prc->cr', fitted16, three_index, preferred...  181 us
    all_gather x2, waiting for transfers between devices, per_device(): right = lax.all_gather(current, 'gy', axis=0, tiled=True)  80.5 us
    psum x1, blocking collectives, per_device(): lax.psum(jnp.sum(shifted * shifted), ('gx', 'gy')) / (width * width)  40.2 us
    psum x1, blocking collectives, per_device(): shift = lax.psum(local_trace, ('gx', 'gy')) / width  39.5 us
    psum x1, blocking collectives, per_device(): totals = lax.psum(jnp.stack(traces), ('gx', 'gy'))  39.1 us
    all_gather x2, waiting for transfers between devices, per_device(): square_block = lax.all_gather(square, 'gy', axis=0, tiled=True)  38.9 us
    dot_general x2, matrix products, per_device(): jnp.dot(row_panel, right, preferred_element_type=jnp.float32) * scale  27.4 us
  transfers between devices with their start and end apart: 7, of which 6 were waited for; matrix products, arithmetic and copies ran while one was open for 0% of the time, Pallas kernels for 0%

commit v1 on v0

v1 whole, which is shorter than its diff:
```python
import functools

import jax
import jax.numpy as jnp
from jax import lax
from jax.experimental import pallas as pl
from jax.experimental.pallas import tpu as pltpu
from jax.sharding import PartitionSpec as P

ITERS = 2


def ring_index(position, n):
    low = (position < n // 2).astype(jnp.int32)
    return low * (2 * position) + (1 - low) * (2 * (n - 1 - position) + 1)


def gather_kernel(
    n, m, cur_t, cur, panel, right, own_t, own, load_sem, keep_sem, send_sem, recv_sem, col_send, col_recv
):
    gx = lax.axis_index("gx")
    gy = lax.axis_index("gy")
    cols = cur_t.shape[0]
    rows = cur.shape[0]
    odd = lax.rem(gx, 2)
    place = (1 - odd) * (gx // 2) + odd * (n - 1 - gx // 2)
    ahead = ring_index(lax.rem(place + 1, n), n)
    behind = ring_index(lax.rem(place + n - 1, n), n)

    barrier = pltpu.get_barrier_semaphore()
    for other in (ahead, behind):
        pl.semaphore_signal(barrier, inc=1, device_id={"gx": other})
    for k in range(1, m):
        pl.semaphore_signal(barrier, inc=1, device_id={"gy": lax.rem(gy + k, m)})
    pl.semaphore_wait(barrier, m + 1)

    def block(owner):
        return panel.at[pl.ds(pl.multiple_of(owner * cols, cols), cols), :]

    def hop(way, step):
        source = lax.rem(place + (n - step if way == 0 else step), n)
        owner = ring_index(source, n)
        return pltpu.make_async_remote_copy(
            src_ref=cur_t if step == 0 else block(owner),
            dst_ref=block(owner),
            send_sem=send_sem.at[way, step],
            recv_sem=recv_sem.at[way, step],
            device_id={"gx": ahead if way == 0 else behind},
        )

    counts = (n // 2, n - 1 - n // 2)
    hops = [[hop(way, step) for step in range(counts[way])] for way in (0, 1)]
    for way in (0, 1):
        hops[way][0].start()
    mine = right.at[pl.ds(pl.multiple_of(gy * rows, rows), rows), :]
    spread = [
        pltpu.make_async_remote_copy(
            src_ref=cur,
            dst_ref=mine,
            send_sem=col_send.at[k - 1],
            recv_sem=col_recv.at[k - 1],
            device_id={"gy": lax.rem(gy + k, m)},
        )
        for k in range(1, m)
    ]
    for copy in spread:
        copy.start()
    loads = [
        pltpu.make_async_copy(cur_t, own_t, load_sem.at[0]),
        pltpu.make_async_copy(cur, own, load_sem.at[1]),
    ]
    keeps = [
        pltpu.make_async_copy(own_t, block(gx), keep_sem.at[0]),
        pltpu.make_async_copy(own, mine, keep_sem.at[1]),
    ]
    for copy in loads:
        copy.start()
    for load, keep in zip(loads, keeps):
        load.wait()
        keep.start()
    for step in range(counts[0]):
        for way in (0, 1):
            if step < counts[way]:
                hops[way][step].wait_recv()
                if step + 1 < counts[way]:
                    hops[way][step + 1].start()
    for way in (0, 1):
        for copy in hops[way]:
            copy.wait_send()
    for copy in spread:
        copy.wait()
    for keep in keeps:
        keep.wait()


def gather(cur_t, cur, n, m, ident):
    cols, rows = cur_t.shape
    return pl.pallas_call(
        functools.partial(gather_kernel, n, m),
        out_shape=(
            jax.ShapeDtypeStruct((n * cols, rows), cur.dtype),
            jax.ShapeDtypeStruct((m * rows, cols), cur.dtype),
        ),
        in_specs=[pl.BlockSpec(memory_space=pltpu.HBM)] * 2,
        out_specs=(pl.BlockSpec(memory_space=pltpu.HBM),) * 2,
        scratch_shapes=[
            pltpu.VMEM((cols, rows), cur.dtype),
            pltpu.VMEM((rows, cols), cur.dtype),
            pltpu.SemaphoreType.DMA((2,)),
            pltpu.SemaphoreType.DMA((2,)),
            pltpu.SemaphoreType.DMA((2, n // 2)),
            pltpu.SemaphoreType.DMA((2, n // 2)),
            pltpu.SemaphoreType.DMA((m - 1,)),
            pltpu.SemaphoreType.DMA((m - 1,)),
        ],
        compiler_params=pltpu.CompilerParams(collective_id=ident, has_side_effects=True),
    )(cur_t, cur)


def scatter_kernel(n, parts, out, own, sums, landed, load_sem, send_sem, recv_sem):
    gx = lax.axis_index("gx")
    cols = out.shape[0]
    odd = lax.rem(gx, 2)
    place = (1 - odd) * (gx // 2) + odd * (n - 1 - gx // 2)
    ahead = ring_index(lax.rem(place + 1, n), n)
    behind = ring_index(lax.rem(place + n - 1, n), n)
    barrier = pltpu.get_barrier_semaphore()
    for other in (ahead, behind):
        pl.semaphore_signal(barrier, inc=1, device_id={"gx": other})
    pl.semaphore_wait(barrier, 2)

    counts = (n // 2, n - 1 - n // 2)
    starts = (0, n // 2)
    order = [(way, step) for step in range(counts[0]) for way in (0, 1) if step < counts[way]]

    def slot(way, step):
        return starts[way] + step

    def target(way, step):
        far = counts[way] - step
        return ring_index(lax.rem(place + (far if way == 0 else n - far), n), n)

    def load(owner, k):
        return pltpu.make_async_copy(
            parts.at[pl.ds(pl.multiple_of(owner * cols, cols), cols), :], own.at[k], load_sem.at[k]
        )

    def hop(way, step):
        k = slot(way, step)
        return pltpu.make_async_remote_copy(
            src_ref=own.at[k] if step == 0 else sums.at[k],
            dst_ref=landed.at[k],
            send_sem=send_sem.at[k],
            recv_sem=recv_sem.at[k],
            device_id={"gx": ahead if way == 0 else behind},
        )

    loads = {key: load(target(*key), slot(*key)) for key in order}
    loads["mine"] = load(gx, n - 1)
    for copy in loads.values():
        copy.start()
    hops = {key: hop(*key) for key in order}
    tile = next(t for t in (64, 48, 32, 16, 8) if cols % t == 0)
    for way, step in order:
        loads[way, step].wait()
        if step > 0:
            k = slot(way, step)
            hops[way, step - 1].wait_recv()

            @pl.loop(0, cols // tile)
            def _(r):
                at = pl.ds(pl.multiple_of(r * tile, tile), tile)
                total = own[k, at, :].astype(jnp.float32) + landed[k - 1, at, :].astype(jnp.float32)
                sums[k, at, :] = total.astype(sums.dtype)

        hops[way, step].start()
    loads["mine"].wait()
    ends = [slot(way, counts[way] - 1) for way in (0, 1)]
    for way in (0, 1):
        hops[way, counts[way] - 1].wait_recv()

    @pl.loop(0, cols // tile)
    def _(r):
        at = pl.ds(pl.multiple_of(r * tile, tile), tile)
        total = own[n - 1, at, :].astype(jnp.float32)
        for k in ends:
            total = total + landed[k, at, :].astype(jnp.float32)
        out[at, :] = total

    for copy in hops.values():
        copy.wait_send()


def scatter(parts, n, ident):
    cols, rows = parts.shape[0] // n, parts.shape[1]
    return pl.pallas_call(
        functools.partial(scatter_kernel, n),
        out_shape=jax.ShapeDtypeStruct((cols, rows), jnp.float32),
        in_specs=[pl.BlockSpec(memory_space=pltpu.HBM)],
        out_specs=pl.BlockSpec(memory_space=pltpu.VMEM),
        scratch_shapes=[
            pltpu.VMEM((n, cols, rows), parts.dtype),
            pltpu.VMEM((n - 1, cols, rows), parts.dtype),
            pltpu.VMEM((n - 1, cols, rows), parts.dtype),
            pltpu.SemaphoreType.DMA((n,)),
            pltpu.SemaphoreType.DMA((n - 1,)),
            pltpu.SemaphoreType.DMA((n - 1,)),
        ],
        compiler_params=pltpu.CompilerParams(
            collective_id=ident, has_side_effects=True, vmem_limit_bytes=48 * 1024 * 1024
        ),
    )(parts)


def merge_kernel(n, m, x_ref, o_ref, held, landed, send_sem, recv_sem):
    partners = []
    for axis, size in (("gy", m), ("gx", n)):
        me = lax.axis_index(axis)
        bit = 1
        while bit < size:
            partners.append({axis: me + bit * (1 - 2 * lax.rem(me // bit, 2))})
            bit *= 2
    barrier = pltpu.get_barrier_semaphore()
    for other in partners:
        pl.semaphore_signal(barrier, inc=1, device_id=other)
    pl.semaphore_wait(barrier, len(partners))
    held[0] = x_ref[...]
    for k, other in enumerate(partners):
        copy = pltpu.make_async_remote_copy(
            src_ref=held.at[k],
            dst_ref=landed.at[k],
            send_sem=send_sem.at[k],
            recv_sem=recv_sem.at[k],
            device_id=other,
        )
        copy.start()
        copy.wait()
        a, b = held[k], landed[k]
        gap = a[1] / jnp.maximum(a[2], 1.0) - b[1] / jnp.maximum(b[2], 1.0)
        weight = a[2] * b[2] / jnp.maximum(a[2] + b[2], 1.0)
        held[k + 1, 0] = a[0] + b[0] + weight * (gap * gap)
        held[k + 1, 1] = a[1] + b[1]
        held[k + 1, 2] = a[2] + b[2]
    o_ref[...] = held[len(partners)]


def merge(squares, total, count, n, m, ident):
    x = jnp.broadcast_to(
        jnp.stack([squares, total, count]).astype(jnp.float32)[:, None, None], (3, 8, 128)
    )
    steps = (n - 1).bit_length() + (m - 1).bit_length()
    out = pl.pallas_call(
        functools.partial(merge_kernel, n, m),
        out_shape=jax.ShapeDtypeStruct(x.shape, x.dtype),
        in_specs=[pl.BlockSpec(memory_space=pltpu.VMEM)],
        out_specs=pl.BlockSpec(memory_space=pltpu.VMEM),
        scratch_shapes=[
            pltpu.VMEM((steps + 1, 3, 8, 128), jnp.float32),
            pltpu.VMEM((steps, 3, 8, 128), jnp.float32),
            pltpu.SemaphoreType.DMA((steps,)),
            pltpu.SemaphoreType.DMA((steps,)),
        ],
        compiler_params=pltpu.CompilerParams(collective_id=ident, has_side_effects=True),
    )(x)
    return out[0, 0, 0], out[1, 0, 0]


def per_device(n, m, three_index, old_density, core):
    aux_dev, rows, width = three_index.shape
    cols = core.shape[1]
    dens = old_density.astype(jnp.float32)
    partial_value = jnp.sum(three_index.astype(jnp.float32) * dens[None], axis=(1, 2))
    fitted = lax.psum(partial_value, "gy")
    fitted16 = fitted.astype(jnp.bfloat16)
    parts = jnp.einsum(
        "p,prc->cr", fitted16, three_index, preferred_element_type=jnp.float32
    ).astype(jnp.bfloat16)
    coulomb = scatter(parts, n, 2 + ITERS)
    fock = core + coulomb.T
    row_start = lax.axis_index("gy") * rows
    col_start = lax.axis_index("gx") * cols
    row_ids = row_start + lax.broadcasted_iota(jnp.int32, (rows, cols), 0)
    col_ids = col_start + lax.broadcasted_iota(jnp.int32, (rows, cols), 1)
    diagonal = row_ids == col_ids
    diag_mask = diagonal.astype(jnp.float32)
    count = jnp.maximum(
        jnp.minimum(row_start + rows, col_start + cols) - jnp.maximum(row_start, col_start), 0
    ).astype(jnp.float32)
    local_trace = jnp.sum(jnp.where(diagonal, fock, 0.0))
    centred = fock - (local_trace / jnp.maximum(count, 1.0)) * diag_mask
    squares, trace = merge(jnp.sum(centred * centred), local_trace, count, n, m, 0)
    shift = trace / width
    spread = squares / (width * width)
    current = ((shift * diag_mask - fock) / (4.0 * jnp.sqrt(spread + 1e-06))).astype(jnp.bfloat16)
    scale = 1.0 / jnp.sqrt(jnp.float32(width))
    contract = (((0,), (0,)), ((), ()))
    traces = []
    for step in range(ITERS):
        panel, right = gather(current.T, current, n, m, 1 + step)
        square_full = lax.dot_general(panel, right, contract, preferred_element_type=jnp.float32) * scale
        square = square_full.astype(jnp.bfloat16)
        square_block = lax.all_gather(square, "gy", axis=0, tiled=True)
        cube = lax.dot_general(panel, square_block, contract, preferred_element_type=jnp.float32) * scale
        traces.append(jnp.sum(jnp.where(diagonal, square_full, 0.0)))
        current = (1.5 * current.astype(jnp.float32) - 2.0 * cube).astype(jnp.bfloat16)
    last, first = merge(traces[1], traces[0], jnp.float32(0), n, m, 1 + ITERS)
    idempotency = 16.0 * (0.25 - jnp.stack([first, last]) / (width * jnp.sqrt(jnp.float32(width))))
    return (current, idempotency)


def solution(mesh):
    placed = (P("gx", "gy", None), P("gy", None), P("gy", "gx"))
    return jax.shard_map(
        functools.partial(per_device, mesh.shape["gx"], mesh.shape["gy"]),
        mesh=mesh,
        in_specs=placed,
        out_specs=(P("gy", "gx"), P()),
        check_vma=False,
    )
```

time: 897 us -> 624 us (0.70)
  waiting for transfers between devices: 611 us -> 65.1 us
  Pallas kernels: 0 us -> 393 us
  blocking collectives: 128 us -> 8.99 us
    pallas_call x0 -> x5, Pallas kernels: none -> 393 us  [the longest x2 242 us: gather(): pl.pallas_call(functools.partial(gather_kernel, n, m), out_shape=(jax.Sha...]
    all_gather x4 -> x0, waiting for transfers between devices: 390 us -> none  [the longest x2 310 us: per_device(): row_panel = lax.all_gather(current, 'gx', axis=1, tiled=True)]
    reduce_scatter x1 -> x0, waiting for transfers between devices: 181 us -> none  [per_device(): lax.psum_scatter(jnp.einsum('p,prc->cr', fitted16, three_index, preferred...]
    psum x3 -> x0, blocking collectives: 119 us -> none  [the longest x1 40.2 us: per_device(): lax.psum(jnp.sum(shifted * shifted), ('gx', 'gy')) / (width * width)]
    reshape x2 -> x0, local copies, waits for them, and re-layouts: 39.6 us -> none  [the longest x1 19.8 us: per_device(): old_density.reshape(rows * width)]
    all_gather x2, waiting for transfers between devices: 38.9 us -> 65.1 us  [per_device(): square_block = lax.all_gather(square, 'gy', axis=0, tiled=True)]
    unnamed x7 -> x12, local copies, waits for them, and re-layouts: 15.3 us -> 36 us
    reduce_sum x2 -> x3, other arithmetic: 5.73 us -> 17.5 us  [the longest x1 10.7 us: per_device(): jnp.sum(three_index.astype(jnp.float32) * dens[None], axis=(1, 2))]
  transfers between devices with their start and end apart: 7 -> 2, of which waited for: 6 -> 2; matrix products, arithmetic and copies ran while one was open for 0% -> 1% of each run, Pallas kernels for 0% -> 2%
where the time goes in v1:
time: 624 us; the launch traced here: 623 us
  Pallas kernels  393 us (63%)
  waiting for transfers between devices  65.1 us (10%)
  matrix products  56 us (9%)
  local copies, waits for them, and re-layouts  46.5 us (7%)
  other arithmetic  36.1 us (6%)
  between operations  16.8 us (3%)
  blocking collectives  8.99 us (1%)
    pallas_call x2, Pallas kernels, gather(): pl.pallas_call(functools.partial(gather_kernel, n, m), out_shape=(jax.Sha...  242 us
    pallas_call x1, Pallas kernels, scatter(): pl.pallas_call(functools.partial(scatter_kernel, n), out_shape=jax.ShapeD...  119 us
    all_gather x2, waiting for transfers between devices, per_device(): square_block = lax.all_gather(square, 'gy', axis=0, tiled=True)  65.1 us
    unnamed x12, local copies, waits for them, and re-layouts  36 us
    pallas_call x2, Pallas kernels, merge(): pl.pallas_call(functools.partial(merge_kernel, n, m), out_shape=jax.Shape...  31.9 us
    dot_general x2, matrix products, per_device(): lax.dot_general(panel, right, contract, preferred_element_type=jnp.float32)  30.9 us
    dot_general x2, matrix products, per_device(): lax.dot_general(panel, square_block, contract, preferred_element_type=jnp...  25.2 us
  transfers between devices with their start and end apart: 2, of which 2 were waited for; matrix products, arithmetic and copies ran while one was open for 1% of the time, Pallas kernels for 2%

profile of v1, /device:TPU:0, one launch (start us, length us, event | category | flops | bytes accessed | tf_op | source)
XLA Modules:
  0.0 622.6 jit_solution(5149491460472941716)
XLA Ops:
  7.2 0.0 all-gather.3.cloned.1.call-start
  7.2 15.3 %copy.5 = bf16[1,1152,4608]{1,2,0:T(8,128)(2,1)} copy(bf16[1,1152,4608]{2,1,0:T(8,128)(2,1)} %param.3) | data formatting | bytes 21233664 | tf_op args[0]
  22.6 15.2 %copy.6 = bf16[1152,4608]{0,1:T(8,128)(2,1)} copy(bf16[1152,4608]{1,0:T(8,128)(2,1)} %param.4) | data formatting | bytes 21233664 | tf_op args[1]
  37.8 10.7 %fusion = f32[]{:T(128)} fusion(bf16[1,1152,4608]{1,2,0:T(8,128)(2,1)} %copy.5, bf16[1152,4608]{0,1:T(8,128)(2,1)} %copy.6), kind=kLoop, calls=%fused_computation.2 | loop fusion | flops 21233664 | bytes 21233668 | tf_op jit(solution)/shard_map/reduce_sum | solution.py:272
  48.5 9.0 %psum.7 = bf16[1]{0:T(256)(128)(2,1)} all-reduce(f32[1]{0:T(128)} %bitcast.1), channel_id=1, replica_groups=mesh['gx'=8,'gy'=4] {'gy'}, use_global_device_ids=true, to_apply=%region_1.0 | all-reduce | flops 1 | bytes 6 | tf_op jit(solution)/shard_map/psum | solution.py:273
  58.2 10.5 %fusion.2.parts = bf16[4608,1152]{1,0:T(8,128)(2,1)} fusion(bf16[1,1152,4608]{1,2,0:T(8,128)(2,1)} %copy.5, f32[]{:T(128)S(6)} %convert.11), kind=kLoop, calls=%fused_computation.4 | loop fusion | flops 15925248 | bytes 21233668 | tf_op jit(solution)/shard_map/convert_element_type | solution.py:277
  68.7 118.6 %shard_map.50 = f32[576,1152]{1,0:T(8,128)S(1)} custom-call(bf16[4608,1152]{1,0:T(8,128)(2,1)} %fusion.2.parts), custom_call_target="tpu_custom_call" | custom-call | tf_op jit(solution)/shard_map/pallas_call | solution.py:196
  187.3 2.4 copy.7
  189.7 0.0 copy-start
  189.7 3.6 copy.8
  193.3 0.0 copy-done
  193.3 3.3 fusion.7
  197.3 3.4 fusion.10
  200.7 1.3 pad_maximum_fusion
  202.0 0.7 broadcast_in_dim.27.x_ref
  202.7 17.5 %shard_map.51 = f32[3,8,128]{2,1,0:T(8,128)} custom-call(f32[3,8,128]{2,1,0:T(8,128)} %broadcast_in_dim.27.x_ref), custom_call_target="tpu_custom_call" | custom-call | tf_op jit(solution)/shard_map/pallas_call | solution.py:252
  220.2 1.2 fusion.19
  222.7 3.5 fusion.15.cur
  226.3 2.6 copy.9.cur_t
  228.8 120.3 %shard_map.52 = (bf16[4608,1152]{1,0:T(8,128)(2,1)}, bf16[4608,576]{1,0:T(8,128)(2,1)}) custom-call(bf16[576,1152]{1,0:T(8,128)(2,1)} %copy.9.cur_t, bf16[1152,576]{1,0:T(8,128)(2,1)} %fusion.15.cur), custom_call_target="tpu_custom_call" | custom-call | tf_op jit(solution)/shard_map/pallas_call | solution.py:98
  349.1 0.0 copy-start.1
  349.1 14.6 %fusion.20 = (bf16[1152,576]{1,0:T(8,128)(2,1)}, f32[1152,576]{1,0:T(8,128)}) fusion(bf16[4608,1152]{1,0:T(8,128)(2,1)} %get-tuple-element.6, bf16[4608,576]{1,0:T(8,128)(2,1)} %get-tuple-element.7), kind=kOutput, calls=%fused_computation.37 | convolution fusion | flops 6116622336 | bytes 19906560 | tf_op jit(solution)/shard_map/dot_general | solution.py:300
  363.7 0.0 all-gather.3.cloned.1.call-update
  363.7 0.2 all-gather.5.cloned.1.call-start
  363.9 43.1 %all-gather.3.cloned.1.call-done = bf16[4608,576]{1,0:T(8,128)(2,1)} async-done(((bf16[1152,576]{1,0:T(8,128)(2,1)}), bf16[4608,576]{1,0:T(8,128)(2,1)}) %all-gather.3.cloned.1.call-update) | async-done | bytes 5308432 | tf_op jit(solution)/shard_map/all_gather | solution.py:302
  407.0 0.0 copy-done.1
  407.0 12.6 %fusion.6.cur = bf16[1152,576]{1,0:T(8,128)(2,1)S(1)} fusion(bf16[4608,1152]{1,0:T(8,128)(2,1)} %get-tuple-element.6, bf16[4608,576]{1,0:T(8,128)(2,1)} %all-gather.3.cloned.1.call-done, bf16[1152,576]{1,0:T(8,128)(2,1)S(1)} %copy-done.1), kind=kOutput, calls=%fused_computation.17 | convolution fusion | flops 6118612992 | bytes 18579456 | tf_op jit(solution)/shard_map/dot_general | solution.py:303
  419.6 0.0 copy-start.2
  419.6 1.8 copy.12.cur_t
  421.4 0.0 copy-done.2
  421.4 122.2 %shard_map.53 = (bf16[4608,1152]{1,0:T(8,128)(2,1)}, bf16[4608,576]{1,0:T(8,128)(2,1)}) custom-call(bf16[576,1152]{1,0:T(8,128)(2,1)} %copy.12.cur_t, bf16[1152,576]{1,0:T(8,128)(2,1)} %copy-done.2), custom_call_target="tpu_custom_call" | custom-call | tf_op jit(solution)/shard_map/pallas_call | solution.py:98
  543.6 0.0 copy-start.3
  543.6 16.3 %fusion.13 = (f32[]{:T(128)}, f32[]{:T(128)}, bf16[1152,576]{1,0:T(8,128)(2,1)}) fusion(s32[576]{0:T(1024)S(1)} %iota_add_fusion.1, s32[1152]{0:T(1024)S(1)} %iota_add_fusion, f32[1152,576]{1,0:T(8,128)} %get-tuple-element.20, bf16[4608,1152]{1,0:T(8,128)(2,1)} %get-tuple-element.8, bf16[4608,576]{1,0:T(8,128)(2,1)} %get-tuple-element.9), kind=kOutput, calls=%fused_computation.24 | convolution fusion | flops 6119940096 | bytes 19913480 | tf_op jit(solution)/shard_map/dot_general | solution.py:300
  559.9 0.0 all-gather.5.cloned.1.call-update
  559.9 1.4 pad_maximum_fusion.1
  561.3 0.7 broadcast_in_dim.28.x_ref
  562.0 14.4 %shard_map.54 = f32[3,8,128]{2,1,0:T(8,128)} custom-call(f32[3,8,128]{2,1,0:T(8,128)} %broadcast_in_dim.28.x_ref), custom_call_target="tpu_custom_call" | custom-call | tf_op jit(solution)/shard_map/pallas_call | solution.py:252
  576.4 1.2 fusion.18
  577.6 1.9 fusion.17
  579.4 22.0 %all-gather.5.cloned.1.call-done = bf16[4608,576]{1,0:T(8,128)(2,1)} async-done(((bf16[1152,576]{1,0:T(8,128)(2,1)}), bf16[4608,576]{1,0:T(8,128)(2,1)}) %all-gather.5.cloned.1.call-update) | async-done | bytes 5308432 | tf_op jit(solution)/shard_map/all_gather | solution.py:302
  601.4 0.0 copy-done.3
  601.4 12.6 %fusion.5 = bf16[1152,576]{1,0:T(8,128)(2,1)S(1)} fusion(bf16[4608,1152]{1,0:T(8,128)(2,1)} %get-tuple-element.8, bf16[4608,576]{1,0:T(8,128)(2,1)} %all-gather.5.cloned.1.call-done, bf16[1152,576]{1,0:T(8,128)(2,1)S(1)} %copy-done.3), kind=kOutput, calls=%fused_computation.16 | convolution fusion | flops 6118612992 | bytes 18579456 | tf_op jit(solution)/shard_map/dot_general | solution.py:303
  614.0 1.8 copy.15
  (2 shorter events, 0.0 us)
Async XLA Ops:
  7.2 399.9 %all-gather.3.cloned.1.call-start = ((), (), s32[]{:S(2)}) async-start(), calls=%async_computation | async-start | bytes 7372800 | tf_op jit(solution)/shard_map/all_gather | solution.py:302
  189.7 3.6 copy-start
  349.1 57.9 %copy-start.1 = (bf16[1152,576]{1,0:T(8,128)(2,1)S(1)}, bf16[1152,576]{1,0:T(8,128)(2,1)}, u32[]{:S(2)}) copy-start(bf16[1152,576]{1,0:T(8,128)(2,1)} %fusion.15.cur) | copy-start | bytes 3981316
  363.7 237.7 %all-gather.5.cloned.1.call-start = ((), (), s32[]{:S(2)}) async-start(), calls=%async_computation.1 | async-start | bytes 7372800 | tf_op jit(solution)/shard_map/all_gather | solution.py:302
  419.6 1.8 copy-start.2
  543.6 57.8 %copy-start.3 = (bf16[1152,576]{1,0:T(8,128)(2,1)S(1)}, bf16[1152,576]{1,0:T(8,128)(2,1)}, u32[]{:S(2)}) copy-start(bf16[1152,576]{1,0:T(8,128)(2,1)} %copy-done.2) | copy-start | bytes 3981316
Sparse Core Ops, SparseCore 0:
  363.8 43.1 all-gather.2
  560.0 41.3 all-gather.4
